TPU v7x, 768 devices: a whole 4x8x12 slice. The times are simulated.
768 devices in a mesh: rep: 192 (over z, y, core), fsdp: 4 (over x).
Axes of the slice: x: 4, y: 8, z: 12, core: 2. Of those that a mesh axis runs over, the one named last changes fastest.
Arguments:
- activations: bfloat16 [98304, 8192], P(('rep', 'fsdp')), may hold values from -7.153361557201429 to 7.153361557201429
- upstream: bfloat16 [98304, 512], P(('rep', 'fsdp')), may hold values from -0.3161369 to 0.3161369
- q_start: float32 [4, 4, 512], P('fsdp'), may hold values from -6 to 6
Outputs:
- error_feedback: bfloat16 [192, 8192, 512], P('rep', 'fsdp')
- p_basis: float32 [4, 4, 2048], P('fsdp')
- q_factor: float32 [4, 4, 512], P('fsdp')
All inputs are finite; a program needn't handle non-finite values.
Results may differ from a plain program's by a relative error of at most 0.015.
Values may be sent and summed in bfloat16 or wider, within the bound.
No kernel may reach another device: no remote copies, remote signals or barrier semaphores. Data moves between devices by JAX's collectives and lax.ppermute only.
A program may use at most 64 MiB of HBM per device.

v0:
```python
import functools

import jax
import jax.numpy as jnp
from jax import lax
from jax.sharding import Mesh
from jax.sharding import PartitionSpec as P

REP = ("rep_0", "rep_1", "rep_2")
REP_FSDP = ("rep_0", "rep_1", "rep_2", "fsdp")


def sent_to_all(array, axis):
    devices = lax.axis_size(axis)
    return lax.all_to_all(
        jnp.broadcast_to(array[None], (devices, *array.shape)), axis, 0, 0, tiled=True
    )


def joined_along(blocks, dim):
    blocks = jnp.moveaxis(blocks, 0, dim)
    lengths = blocks.shape
    return blocks.reshape(*lengths[:dim], lengths[dim] * lengths[dim + 1], *lengths[dim + 2 :])


def collect(array, axis, dim):
    blocks = sent_to_all(array, axis)
    return joined_along(blocks, dim)


def one_axis_at_a_time(array, axes):
    return functools.reduce(lax.psum, axes, array)


def contract_tokens(left, right):
    return lax.dot_general(
        left, right, (((0,), (0,)), ((), ())), preferred_element_type=jnp.float32
    )


def rounded(term):
    short = lax.optimization_barrier(term.astype(jnp.bfloat16))
    return short.astype(jnp.float32)


def on_device(activations, upstream, q_start):
    high = lax.Precision.HIGHEST
    groups = lax.axis_size("fsdp")
    replicas = lax.axis_size(REP)
    tok_rows = activations.shape[0]
    shard_rows = activations.shape[1] // groups
    columns = lax.all_to_all(activations, "fsdp", split_axis=1, concat_axis=0, tiled=True)
    cotangent_all = collect(upstream, "fsdp", 0)
    shard = jnp.zeros((shard_rows, upstream.shape[1]), jnp.float32)
    for source in range(groups):
        left = columns[source * tok_rows : (source + 1) * tok_rows]
        right = cotangent_all[source * tok_rows : (source + 1) * tok_rows]
        shard = shard + rounded(contract_tokens(left, right))
    q_local = q_start[0]
    left_local = lax.dot_general(
        q_local, shard, (((1,), (1,)), ((), ())), precision=high, preferred_element_type=jnp.float32
    )
    p_sum = one_axis_at_a_time(left_local, REP)
    gram_small = jnp.dot(p_sum, p_sum.T, precision=high) + 1e-06 * jnp.eye(
        p_sum.shape[0], dtype=jnp.float32
    )
    factor = jnp.linalg.cholesky(gram_small)
    p_basis = lax.linalg.triangular_solve(factor, p_sum, left_side=True, lower=True)
    right_local = jnp.dot(p_basis, shard, precision=high)
    q_factor = one_axis_at_a_time(right_local, REP)
    approx = lax.dot_general(
        p_basis,
        q_factor / replicas,
        (((0,), (0,)), ((), ())),
        precision=high,
        preferred_element_type=jnp.float32,
    )
    error_feedback = (shard - approx).astype(jnp.bfloat16)
    return (error_feedback[None], p_basis[None], q_factor[None])


def solution(mesh):
    split = Mesh(
        mesh.devices.reshape(12, 8, 2, mesh.shape["fsdp"]), ("rep_0", "rep_1", "rep_2", "fsdp")
    )
    return jax.shard_map(
        on_device,
        mesh=split,
        in_specs=(P(REP_FSDP, None), P(REP_FSDP, None), P("fsdp", None, None)),
        out_specs=(P(REP, "fsdp", None), P("fsdp", None, None), P("fsdp", None, None)),
        check_vma=False,
    )
```

profile of v0, /device:TPU:1, one launch (start us, length us, event | category | flops | bytes accessed | tf_op | source)
XLA Modules:
  0.0 194.5 jit_solution(1833400884990403462)
XLA Ops:
  0.6 0.0 copy-start
  0.6 1.7 broadcast_in_dim.15
  2.4 4.8 %all-to-all-start.1 = ((bf16[4,128,512]{2,1,0:T(8,128)(2,1)}), bf16[4,128,512]{2,1,0:T(8,128)(2,1)S(1)}, u32[]{:S(2)}, u32[]{:S(2)}) async-start(bf16[4,128,512]{2,1,0:T(8,128)(2,1)} %broadcast_in_dim.15), calls=%async_computation.1 | async-start | bytes 1048576 | tf_op jit(solution)/shard_map/all_to_all | solution.py:15
  7.2 3.2 %copy.10 = bf16[128,8192]{0,1:T(8,128)(2,1)S(1)} copy(bf16[128,8192]{1,0:T(8,128)(2,1)} %param.3) | data formatting | bytes 4194304 | tf_op args[0]
  10.4 3.7 %all-to-all-done.1 = bf16[4,128,512]{2,1,0:T(8,128)(2,1)S(1)} async-done(((bf16[4,128,512]{2,1,0:T(8,128)(2,1)}), bf16[4,128,512]{2,1,0:T(8,128)(2,1)S(1)}, u32[]{:S(2)}, u32[]{:S(2)}) %all-to-all-start.1) | async-done | bytes 524320 | tf_op jit(solution)/shard_map/all_to_all | solution.py:15
  14.2 21.4 %all_to_all.21 = bf16[128,4,2048]{0,2,1:T(8,128)(2,1)S(1)} all-to-all(bf16[128,4,2048]{0,2,1:T(8,128)(2,1)S(1)} %bitcast.56), channel_id=1, replica_groups=mesh['rep_0'=12,'rep_1'=8,'rep_2'=2,'fsdp'=4] {'fsdp'}, dimensions={1} | all-to-all | bytes 4194304 | tf_op jit(solution)/shard_map/all_to_all | solution.py:52
  35.6 0.7 convolution_convert_fusion
  36.3 0.7 convolution_convert_fusion.1
  37.0 0.0 copy-start.1
  37.0 0.7 convolution_convert_fusion.3
  37.7 0.0 copy-start.2
  37.7 0.7 convolution_convert_fusion.2
  38.4 0.0 copy-done.1
  38.4 0.6 copy-done.2
  39.0 0.0 copy-start.3
  39.0 1.3 copy-done.3
  40.3 0.0 copy-done
  40.3 4.5 %convolution_bitcast_fusion = f32[4,2048]{1,0:T(4,128)S(1)} fusion(f32[1,4,512]{2,1,0:T(4,128)S(1)} %copy-done, bf16[2048,512]{1,0:T(8,128)(2,1)S(1)} %convolution_convert_fusion, bf16[2048,512]{1,0:T(8,128)(2,1)S(1)} %convolution_convert_fusion.1, bf16[2048,512]{1,0:T(8,128)(2,1)S(1)} %convolution_convert_fusion.2, ...), kind=kOutput, calls=%fused_computation.7 | convolution fusion | flops 57671680 | bytes 8429568 | tf_op jit(solution)/shard_map/dot_general | solution.py:60
  44.8 48.6 %psum.42 = f32[4,2048]{1,0:T(4,128)S(1)} all-reduce(f32[4,2048]{1,0:T(4,128)S(1)} %convolution_bitcast_fusion), channel_id=1, replica_groups=mesh['rep_0'=12,'rep_1'=8,'rep_2'=2,'fsdp'=4] {'rep_0'}, use_global_device_ids=true, to_apply=%region_0.0 | all-reduce | flops 8192 | bytes 65536 | tf_op jit(solution)/shard_map/psum | solution.py:32
  93.4 23.1 %psum.43 = f32[4,2048]{1,0:T(4,128)S(1)} all-reduce(f32[4,2048]{1,0:T(4,128)S(1)} %psum.42), channel_id=1, replica_groups=mesh['rep_0'=12,'rep_1'=8,'rep_2'=2,'fsdp'=4] {'rep_1'}, use_global_device_ids=true, to_apply=%region_1.0 | all-reduce | flops 8192 | bytes 65536 | tf_op jit(solution)/shard_map/psum | solution.py:32
  116.5 24.1 %psum.44 = f32[4,2048]{1,0:T(4,128)S(1)} all-reduce(f32[4,2048]{1,0:T(4,128)S(1)} %psum.43), channel_id=1, replica_groups=mesh['rep_0'=12,'rep_1'=8,'rep_2'=2,'fsdp'=4] {'rep_2'}, use_global_device_ids=true, to_apply=%region_2.0 | all-reduce | flops 8192 | bytes 65536 | tf_op jit(solution)/shard_map/psum | solution.py:32
  140.6 0.2 fusion.11
  140.8 0.1 copy.15
  140.9 0.4 cholesky.16
  141.4 0.6 compare_reduce_fusion
  142.0 0.6 fusion.4
  142.7 0.3 custom-call.6
  143.0 0.3 fusion.5
  143.3 0.0 copy-start.4
  143.3 5.9 %fusion.10 = f32[4,512]{1,0:T(4,128)S(1)} fusion(f32[4,2048]{1,0:T(4,128)S(1)} %fusion.5, bf16[2048,512]{1,0:T(8,128)(2,1)S(1)} %convolution_convert_fusion, bf16[2048,512]{1,0:T(8,128)(2,1)} %copy-done.1, bf16[2048,512]{1,0:T(8,128)(2,1)} %copy-done.3, bf16[2048,512]{1,0:T(8,128)(2,1)} %copy-done.2), kind=kOutput, calls=%fused_computation.32 | convolution fusion | flops 57671680 | bytes 8429568 | tf_op jit(solution)/shard_map/dot_general | solution.py:69
  149.2 15.8 %psum.45 = f32[4,512]{1,0:T(4,128)S(1)} all-reduce(f32[4,512]{1,0:T(4,128)S(1)} %fusion.10), channel_id=1, replica_groups=mesh['rep_0'=12,'rep_1'=8,'rep_2'=2,'fsdp'=4] {'rep_0'}, use_global_device_ids=true, to_apply=%region_5.6 | all-reduce | flops 2048 | bytes 16384 | tf_op jit(solution)/shard_map/psum | solution.py:32
  165.0 11.3 %psum.46 = f32[4,512]{1,0:T(4,128)S(1)} all-reduce(f32[4,512]{1,0:T(4,128)S(1)} %psum.45), channel_id=1, replica_groups=mesh['rep_0'=12,'rep_1'=8,'rep_2'=2,'fsdp'=4] {'rep_1'}, use_global_device_ids=true, to_apply=%region_6.7 | all-reduce | flops 2048 | bytes 16384 | tf_op jit(solution)/shard_map/psum | solution.py:32
  176.3 10.7 %psum.47 = f32[4,512]{1,0:T(4,128)S(1)} all-reduce(f32[4,512]{1,0:T(4,128)S(1)} %psum.46), channel_id=1, replica_groups=mesh['rep_0'=12,'rep_1'=8,'rep_2'=2,'fsdp'=4] {'rep_2'}, use_global_device_ids=true, to_apply=%region_7.8 | all-reduce | flops 2048 | bytes 16384 | tf_op jit(solution)/shard_map/psum | solution.py:32
  187.0 0.0 copy-done.4
  187.0 0.0 copy-start.5
  187.0 7.5 %fusion = bf16[1,2048,512]{2,1,0:T(8,128)(2,1)} fusion(f32[4,2048]{1,0:T(4,128)S(1)} %fusion.5, f32[4,512]{1,0:T(4,128)S(1)} %psum.47, bf16[2048,512]{1,0:T(8,128)(2,1)S(1)} %convolution_convert_fusion, bf16[2048,512]{1,0:T(8,128)(2,1)} %copy-done.1, bf16[2048,512]{1,0:T(8,128)(2,1)} %copy-done.3, bf16[2048,512]{1,0:T(8,128)(2,1)} %copy-done.2), kind=kOutput, calls=%fused_computation.6 | convolution fusion | flops 59770880 | bytes 10526720 | tf_op jit(solution)/shard_map/dot_general | solution.py:71
  194.5 0.0 copy-done.5
  (2 shorter events, 0.1 us)
Async XLA Ops:
  0.6 39.7 %copy-start = (f32[1,4,512]{2,1,0:T(4,128)S(1)}, f32[1,4,512]{2,1,0:T(4,128)}, u32[]{:S(2)}) copy-start(f32[1,4,512]{2,1,0:T(4,128)} %param.5) | copy-start | bytes 24580
  2.4 11.8 %all-to-all-start.1 = ((bf16[4,128,512]{2,1,0:T(8,128)(2,1)}), bf16[4,128,512]{2,1,0:T(8,128)(2,1)S(1)}, u32[]{:S(2)}, u32[]{:S(2)}) async-start(bf16[4,128,512]{2,1,0:T(8,128)(2,1)} %broadcast_in_dim.15), calls=%async_computation.1 | async-start | bytes 1048576 | tf_op jit(solution)/shard_map/all_to_all | solution.py:15
  37.0 1.4 copy-start.1
  37.7 1.3 copy-start.2
  39.0 1.4 copy-start.3
  143.3 43.7 %copy-start.4 = (f32[4,2048]{1,0:T(4,128)}, f32[4,2048]{1,0:T(4,128)S(1)}, u32[]{:S(2)}) copy-start(f32[4,2048]{1,0:T(4,128)S(1)} %fusion.5) | copy-start | bytes 98308
  187.0 7.5 %copy-start.5 = (f32[4,512]{1,0:T(4,128)}, f32[4,512]{1,0:T(4,128)S(1)}, u32[]{:S(2)}) copy-start(f32[4,512]{1,0:T(4,128)S(1)} %psum.47) | copy-start | bytes 24580
where the time goes:
time: 195 us
  blocking collectives  155 us (79%)
  matrix products  21.2 us (11%)
  local copies, waits for them, and re-layouts  7.01 us (4%)
  starting transfers between devices  4.83 us (2%)
  waiting for transfers between devices  3.71 us (2%)
  other arithmetic  2.09 us (1%)
    psum x6, blocking collectives, one_axis_at_a_time(): return functools.reduce(lax.psum, axes, array)  134 us
    all_to_all x1, blocking collectives, on_device(): lax.all_to_all(activations, 'fsdp', split_axis=1, concat_axis=0, tiled=True)  21.4 us
    dot_general x1, matrix products, on_device(): lax.dot_general(p_basis, q_factor / replicas, (((0,), (0,)), ((), ())), p...  7.54 us
    dot_general x1, matrix products, on_device(): right_local = jnp.dot(p_basis, shard, precision=high)  5.93 us
    unnamed x13, local copies, waits for them, and re-layouts  5.17 us
    all_to_all x1, starting transfers between devices, sent_to_all(): lax.all_to_all(jnp.broadcast_to(array[None], (devices, *array.shape)), ax...  4.83 us
    dot_general x1, matrix products, on_device(): lax.dot_general(q_local, shard, (((1,), (1,)), ((), ())), precision=high,...  4.49 us
  transfers between devices with their start and end apart: 1, of which 1 were waited for; matrix products, arithmetic and copies ran while one was open for 2% of the time, Pallas kernels for 0%

commit v1 on v0

v1 whole, which is shorter than its diff:
```python
import jax
import jax.numpy as jnp
from jax import lax
from jax.experimental import pallas as pl
from jax.experimental.pallas import tpu as pltpu
from jax.sharding import Mesh
from jax.sharding import PartitionSpec as P

REP = ("rep_0", "rep_1", "rep_2")
REP_FSDP = ("rep_0", "rep_1", "rep_2", "fsdp")
VMEM = pl.BlockSpec(memory_space=pltpu.VMEM)
NN = (((1,), (0,)), ((), ()))
NT = (((1,), (1,)), ((), ()))
F32 = jnp.float32
BF16 = jnp.bfloat16


def exchange(array, axis):
    return lax.all_to_all(array, axis, 0, 0, tiled=True)


def sent_to_all(array, axis):
    return exchange(jnp.broadcast_to(array[None], (lax.axis_size(axis), *array.shape)), axis)


def pieces(value):
    first = value.astype(BF16)
    rest = value - first.astype(F32)
    second = rest.astype(BF16)
    third = (rest - second.astype(F32)).astype(BF16)
    return first, second, third


def exact_dot(value, short, dims):
    rows = value.shape[0]
    stacked = jnp.concatenate([p.astype(F32) for p in pieces(value)], axis=0).astype(BF16)
    out = lax.dot_general(stacked, short, dims, preferred_element_type=F32)
    return out[:rows] + (out[rows : 2 * rows] + out[2 * rows :])


def turn_kernel(me_ref, act_ref, up_ref, *refs):
    del me_ref
    groups = len(refs) - 2
    out_refs, held_ref, sems = refs[:groups], refs[-2], refs[-1]
    rows = act_ref.shape[1]
    step = pl.program_id(0)
    held_ref[step, :rows] = act_ref[...].T
    held_ref[step, rows:] = up_ref[...].T
    for k in range(groups):
        copy = pltpu.make_async_copy(held_ref.at[k], out_refs[k], sems.at[k])
        pl.when(step == k)(copy.start)
        pl.when(step == groups - 1)(copy.wait)


def turned(me, activations, upstream, groups):
    tok, width = activations.shape
    rows, cols = width // groups, upstream.shape[1]
    chunk = jax.ShapeDtypeStruct((rows + cols, tok), BF16)
    return pl.pallas_call(
        turn_kernel,
        grid_spec=pltpu.PrefetchScalarGridSpec(
            num_scalar_prefetch=1,
            grid=(groups,),
            in_specs=[
                pl.BlockSpec((tok, rows), lambda k, me_ref: (0, lax.rem(me_ref[0] + k, groups))),
                pl.BlockSpec((tok, cols), lambda k, me_ref: (0, 0)),
            ],
            out_specs=[pl.BlockSpec(memory_space=pl.ANY)] * groups,
            scratch_shapes=[
                pltpu.VMEM((groups, rows + cols, tok), BF16),
                pltpu.SemaphoreType.DMA((groups,)),
            ],
        ),
        out_shape=[chunk] * groups,
        name="turn",
    )(me, activations, upstream)


def left_kernel(me_ref, q_ref, *refs):
    chunk_refs, out_ref = refs[:-1], refs[-1]
    blocks, groups, rank, size = out_ref.shape
    rows = blocks * size
    ups = chunk_refs[0][rows:]
    for k in range(groups):
        g = lax.rem(me_ref[0] + k, groups)
        weights = exact_dot(q_ref[g], ups, NN)
        left = exact_dot(weights, chunk_refs[k][:rows], NT)
        for b in range(blocks):
            out_ref[b, g] = left[:, b * size : (b + 1) * size]


def left_parts(me, q_all, chunks, blocks):
    groups, rank, cols = q_all.shape
    rows = chunks[0].shape[0] - cols
    return pl.pallas_call(
        left_kernel,
        in_specs=[pl.BlockSpec(memory_space=pltpu.SMEM)] + [VMEM] * (groups + 1),
        out_specs=VMEM,
        out_shape=jax.ShapeDtypeStruct((blocks, groups, rank, rows // blocks), F32),
        name="left",
    )(me, q_all, *chunks)


def right_kernel(p_ref, *refs):
    chunk_refs, basis_ref, right_ref = refs[:-2], refs[-2], refs[-1]
    blocks, rank, size = p_ref.shape
    rows = blocks * size
    basis = []
    for i in range(rank):
        vec = p_ref[:, i, :]
        for prev in basis:
            vec = vec - jnp.sum(vec * prev, keepdims=True) * prev
        vec = vec / jnp.sqrt(jnp.sum(vec * vec, keepdims=True) + 1e-06)
        basis.append(vec)
        for b in range(blocks):
            basis_ref[i : i + 1, b * size : (b + 1) * size] = vec[b : b + 1]
    whole = basis_ref[...]
    total = jnp.zeros(right_ref.shape, F32)
    for chunk_ref in chunk_refs:
        weights = exact_dot(whole, chunk_ref[:rows], NN)
        total = total + exact_dot(weights, chunk_ref[rows:], NT)
    right_ref[...] = total


def basis_and_right(p_blocks, chunks):
    blocks, rank, size = p_blocks.shape
    rows = blocks * size
    return pl.pallas_call(
        right_kernel,
        in_specs=[VMEM] * (1 + len(chunks)),
        out_specs=[VMEM] * 2,
        out_shape=[
            jax.ShapeDtypeStruct((rank, rows), F32),
            jax.ShapeDtypeStruct((rank, chunks[0].shape[0] - rows), F32),
        ],
        name="right",
    )(p_blocks, *chunks)


def last_kernel(scale, parts_ref, basis_ref, *refs):
    groups = len(refs) // 2 - 1
    chunk_refs, up_refs = refs[:groups], refs[groups : 2 * groups]
    error_ref, factor_ref = refs[2 * groups :]
    factor = parts_ref[0]
    for part in range(1, parts_ref.shape[0]):
        factor = factor + parts_ref[part]
    factor_ref[...] = factor
    acts = jnp.concatenate([ref[...] for ref in chunk_refs], axis=1)
    ups = jnp.concatenate([ref[...] for ref in up_refs], axis=1)
    grad = lax.dot_general(acts, ups, NT, preferred_element_type=F32)
    b0, b1, b2 = (p.astype(F32) for p in pieces(basis_ref[...]))
    q0, q1, q2 = (p.astype(F32) for p in pieces(factor * scale))
    lefts = jnp.concatenate([b0, b0, b1, b0, b1, b2], axis=0).astype(BF16)
    rights = jnp.concatenate([q0, q1, q0, q2, q1, q0], axis=0).astype(BF16)
    approx = lax.dot_general(lefts, rights, (((0,), (0,)), ((), ())), preferred_element_type=F32)
    error_ref[...] = (grad - approx).astype(BF16)


def error_and_factor(parts, basis, chunks, replicas):
    groups = len(chunks)
    height, tok = chunks[0].shape
    rank, rows = basis.shape
    cols = height - rows
    steps = 4
    step_rows = rows // steps

    def kernel(*refs):
        last_kernel(1.0 / replicas, *refs)

    return pl.pallas_call(
        kernel,
        grid=(steps,),
        in_specs=[
            pl.BlockSpec(parts.shape, lambda s: (0, 0, 0)),
            pl.BlockSpec((rank, step_rows), lambda s: (0, s)),
        ]
        + [pl.BlockSpec((step_rows, tok), lambda s: (s, 0))] * groups
        + [pl.BlockSpec((cols, tok), lambda s: (rows // cols, 0))] * groups,
        out_specs=[
            pl.BlockSpec((step_rows, cols), lambda s: (s, 0)),
            pl.BlockSpec((rank, cols), lambda s: (0, 0)),
        ],
        out_shape=[
            jax.ShapeDtypeStruct((rows, cols), BF16),
            jax.ShapeDtypeStruct((rank, cols), F32),
        ],
        name="last",
    )(parts, basis, *chunks, *chunks)


def on_device(activations, upstream, q_start):
    groups = lax.axis_size("fsdp")
    replicas = lax.axis_size(REP)
    pairs = ("rep_1", "rep_2")
    blocks = lax.axis_size(pairs)
    rank = q_start.shape[1]
    me = lax.axis_index("fsdp")[None]
    q_all = sent_to_all(q_start[0], "fsdp")
    chunks = turned(me, activations, upstream, groups)
    parts = left_parts(me, q_all, chunks, blocks)
    size = parts.shape[-1]
    parts = exchange(parts.reshape(blocks * groups, rank, size), ("rep_1", "rep_2", "fsdp"))
    parts, sent = lax.optimization_barrier((parts, chunks[1:]))
    chunks = [chunks[0]] + [
        lax.ppermute(chunk, "fsdp", [(i, (i + k + 1) % groups) for i in range(groups)])
        for k, chunk in enumerate(sent)
    ]
    mine = jnp.sum(parts, axis=0)
    mine = jnp.sum(sent_to_all(mine, "rep_0"), axis=0)
    p_blocks = sent_to_all(mine, pairs)
    p_basis, right = basis_and_right(p_blocks, chunks)
    right = jnp.sum(sent_to_all(right, "rep_0"), axis=0)
    right_parts = sent_to_all(right, pairs)
    error_feedback, q_factor = error_and_factor(right_parts, p_basis, chunks, replicas)
    return (error_feedback[None], p_basis[None], q_factor[None])


def solution(mesh):
    split = Mesh(
        mesh.devices.reshape(12, 8, 2, mesh.shape["fsdp"]), ("rep_0", "rep_1", "rep_2", "fsdp")
    )
    return jax.shard_map(
        on_device,
        mesh=split,
        in_specs=(P(REP_FSDP, None), P(REP_FSDP, None), P("fsdp", None, None)),
        out_specs=(P(REP, "fsdp", None), P("fsdp", None, None), P("fsdp", None, None)),
        check_vma=False,
    )
```

time: 195 us -> 125 us (0.64)
  blocking collectives: 155 us -> 87.2 us
  matrix products: 21.2 us -> 0 us
  Pallas kernels: 0 us -> 17.9 us
  starting transfers between devices: 4.83 us -> 13.8 us
  waiting for transfers between devices: 3.71 us -> 0.01 us
  local copies, waits for them, and re-layouts: 7.01 us -> 4.6 us
  other arithmetic: 2.09 us -> 0.13 us
    psum x6 -> x0, blocking collectives: 134 us -> none  [one_axis_at_a_time(): return functools.reduce(lax.psum, axes, array)]
    all_to_all x1 -> x5, blocking collectives: 21.4 us -> 87.2 us  [exchange(): return lax.all_to_all(array, axis, 0, 0, tiled=True)]
    dot_general x8 -> x0, matrix products: 20.9 us -> none  [the longest x1 7.54 us: on_device(): lax.dot_general(p_basis, q_factor / replicas, (((0,), (0,)), ((), ())), p...]
    pallas_call x0 -> x4, Pallas kernels: none -> 17.9 us  [the longest x1 5.42 us: error_and_factor(): pl.pallas_call(kernel, grid=(steps,), in_specs=[pl.BlockSpec(parts.shape,...]
    ppermute x0 -> x3, starting transfers between devices: none -> 8.95 us  [on_device(): lax.ppermute(chunk, 'fsdp', [(i, (i + k + 1) % groups) for i in range(gro...]
    all_to_all x1, waiting for transfers between devices: 3.71 us -> 0.01 us  [exchange(): return lax.all_to_all(array, axis, 0, 0, tiled=True)]
    unnamed x13 -> x12, local copies, waits for them, and re-layouts: 5.17 us -> 2.53 us
    another operation x5 -> x0, other arithmetic: 2.08 us -> none  [the longest x3 1.09 us: on_device(): factor = jnp.linalg.cholesky(gram_small)]
  transfers between devices with their start and end apart: 1 -> 4, of which waited for: 1 -> 0; matrix products, arithmetic and copies ran while one was open for 2% -> 0% of each run, Pallas kernels for 0% -> 4%
where the time goes in v1:
time: 125 us; the launch traced here: 124 us
  blocking collectives  87.2 us (70%)
  Pallas kernels  17.9 us (14%)
  starting transfers between devices  13.8 us (11%)
  local copies, waits for them, and re-layouts  4.6 us (4%)
    all_to_all x5, blocking collectives, exchange(): return lax.all_to_all(array, axis, 0, 0, tiled=True)  87.2 us
    ppermute x3, starting transfers between devices, on_device(): lax.ppermute(chunk, 'fsdp', [(i, (i + k + 1) % groups) for i in range(gro...  8.95 us
    pallas_call x1, Pallas kernels, error_and_factor(): pl.pallas_call(kernel, grid=(steps,), in_specs=[pl.BlockSpec(parts.shape,...  5.42 us
    all_to_all x1, starting transfers between devices, exchange(): return lax.all_to_all(array, axis, 0, 0, tiled=True)  4.83 us
    pallas_call x1, Pallas kernels, turned(): pl.pallas_call(turn_kernel, grid_spec=pltpu.PrefetchScalarGridSpec(num_sc...  4.71 us
    pallas_call x1, Pallas kernels, basis_and_right(): pl.pallas_call(right_kernel, in_specs=[VMEM] * (1 + len(chunks)), out_spe...  4.27 us
    pallas_call x1, Pallas kernels, left_parts(): pl.pallas_call(left_kernel, in_specs=[pl.BlockSpec(memory_space=pltpu.SME...  3.46 us
    unnamed x12, local copies, waits for them, and re-layouts  2.53 us
  transfers between devices with their start and end apart: 4, of which 0 were waited for; matrix products, arithmetic and copies ran while one was open for 0% of the time, Pallas kernels for 4%

profile of v1, /device:TPU:1, one launch (start us, length us, event | category | flops | bytes accessed | tf_op | source)
XLA Modules:
  0.0 124.3 jit_solution(13271567617910769618)
XLA Ops:
  0.6 1.3 %broadcast_in_dim.22 = f32[4,4,512]{2,1,0:T(4,128)} broadcast(f32[4,512]{1,0:T(4,128)} %bitcast.8), dimensions={1,2} | broadcast | bytes 40960 | tf_op jit(solution)/shard_map/broadcast_in_dim | solution.py:23
  1.9 4.8 %all-to-all-start = ((f32[4,4,512]{2,1,0:T(4,128)}), f32[4,4,512]{2,1,0:T(4,128)S(1)}, u32[]{:S(2)}, u32[]{:S(2)}) async-start(f32[4,4,512]{2,1,0:T(4,128)} %broadcast_in_dim.22), calls=%async_computation | async-start | bytes 65536 | tf_op jit(solution)/shard_map/all_to_all | solution.py:19
  6.8 4.7 %turn.1 = (bf16[2560,128]{1,0:T(8,128)(2,1)}, bf16[2560,128]{1,0:T(8,128)(2,1)}, bf16[2560,128]{1,0:T(8,128)(2,1)}, bf16[2560,128]{1,0:T(8,128)(2,1)}) custom-call(s32[1]{0:T(128)} %bitcast.me_ref, bf16[128,8192]{1,0:T(8,128)(2,1)} %act_ref.1, bf16[128,512]{1,0:T(8,128)(2,1)} %up_ref.1), custom_call_target="tpu_custom_call" | custom-call | tf_op jit(solution)/shard_map/turn/pallas_call | solution.py:59
  11.5 0.0 copy-start.4
  11.5 0.0 copy-start.3
  11.5 0.0 all-to-all-done.q_ref
  11.5 0.0 copy-start.5
  11.5 0.6 copy-done.5
  12.1 3.5 %left.1 = f32[16,4,4,128]{3,2,1,0:T(4,128)} custom-call(s32[1]{0:T(128)} %bitcast.me_ref, f32[4,4,512]{2,1,0:T(4,128)} %copy-done.5, bf16[2560,128]{1,0:T(8,128)(2,1)} %get-tuple-element.15.refs_0_.refs_2_.refs_6_, bf16[2560,128]{1,0:T(8,128)(2,1)} %get-tuple-element.20.refs_1_, bf16[2560,128]{1,0:T(8,128)(2,1)} %get-tuple-element.21.refs_2_, ...), custom_call_target="tpu_custom_call" | custom-call | tf_op jit(solution)/shard_map/left/pallas_call | solution.py:95
  15.6 24.3 %all_to_all.30 = f32[64,4,128]{2,1,0:T(4,128)S(1)} all-to-all(f32[64,4,128]{2,1,0:T(4,128)} %bitcast.6), channel_id=1, replica_groups=mesh['rep_0'=12,'rep_1'=8,'rep_2'=2,'fsdp'=4] {'rep_1','rep_2','fsdp'}, dimensions={0} | all-to-all | bytes 262144 | tf_op jit(solution)/shard_map/all_to_all | solution.py:19
  39.9 2.2 %collective-permute-start = (bf16[2560,128]{1,0:T(8,128)(2,1)}, bf16[2560,128]{1,0:T(8,128)(2,1)S(1)}, u32[]{:S(2)}, u32[]{:S(2)}) collective-permute-start(bf16[2560,128]{1,0:T(8,128)(2,1)} %get-tuple-element.20.refs_1_), channel_id=1, source_target_pairs={{0,1},{1,2},{2,3},{3,0},{4,5},{5,6},{6,7},{7,4},{8,9},{9,10},{10,1... | collective-permute-start | bytes 1966088 | tf_op jit(solution)/shard_map/ppermute | solution.py:205
  42.1 0.0 copy-done.4
  42.1 4.0 %collective-permute-start.1 = (bf16[2560,128]{1,0:T(8,128)(2,1)S(1)}, bf16[2560,128]{1,0:T(8,128)(2,1)S(1)}, u32[]{:S(2)}, u32[]{:S(2)}) collective-permute-start(bf16[2560,128]{1,0:T(8,128)(2,1)S(1)} %copy-done.4), channel_id=1, source_target_pairs={{0,2},{1,3},{2,0},{3,1},{4,6},{5,7},{6,4},{7,5},{8,10},{9,11},{10,... | collective-permute-start | bytes 1966088 | tf_op jit(solution)/shard_map/ppermute | solution.py:205
  46.2 0.0 copy-done.3
  46.2 2.7 %collective-permute-start.2 = (bf16[2560,128]{1,0:T(8,128)(2,1)S(1)}, bf16[2560,128]{1,0:T(8,128)(2,1)S(1)}, u32[]{:S(2)}, u32[]{:S(2)}) collective-permute-start(bf16[2560,128]{1,0:T(8,128)(2,1)S(1)} %copy-done.3), channel_id=1, source_target_pairs={{0,3},{1,0},{2,1},{3,2},{4,7},{5,4},{6,5},{7,6},{8,11},{9,8},{10,9... | collective-permute-start | bytes 1966088 | tf_op jit(solution)/shard_map/ppermute | solution.py:205
  48.9 0.1 reduce_sum.27
  49.0 21.3 %all_to_all.31 = f32[12,4,128]{2,1,0:T(4,128)S(1)} all-to-all(f32[12,4,128]{2,1,0:T(4,128)S(1)} %broadcast_in_dim.46), channel_id=1, replica_groups=mesh['rep_0'=12,'rep_1'=8,'rep_2'=2,'fsdp'=4] {'rep_0'}, dimensions={0} | all-to-all | bytes 49152 | tf_op jit(solution)/shard_map/all_to_all | solution.py:19
  70.3 14.5 %all_to_all.32.p_ref = f32[16,4,128]{2,1,0:T(4,128)} all-to-all(f32[16,4,128]{2,1,0:T(4,128)S(1)} %broadcast_in_dim.47), channel_id=1, replica_groups=mesh['rep_0'=12,'rep_1'=8,'rep_2'=2,'fsdp'=4] {'rep_1','rep_2'}, dimensions={0} | all-to-all | bytes 65536 | tf_op jit(solution)/shard_map/all_to_all | solution.py:19
  84.8 0.0 collective-permute-done.refs_1_.refs_3_.refs_7_
  84.8 0.0 copy-start
  84.8 0.0 collective-permute-done.1.refs_2_.refs_4_.refs_8_
  84.9 0.0 copy-start.1
  84.9 0.0 collective-permute-done.2.refs_3_.refs_5_.refs_9_
  84.9 0.8 copy-done
  85.7 0.3 copy-done.1
  86.0 0.0 copy-start.2
  86.0 0.8 copy-done.2
  86.8 4.3 %right.1 = (f32[4,2048]{1,0:T(4,128)}, f32[4,512]{1,0:T(4,128)}) custom-call(f32[16,4,128]{2,1,0:T(4,128)} %all_to_all.32.p_ref, bf16[2560,128]{1,0:T(8,128)(2,1)} %get-tuple-element.15.refs_0_.refs_2_.refs_6_, bf16[2560,128]{1,0:T(8,128)(2,1)} %copy-done, bf16[2560,128]{1,0:T(8,128)(2,1)} %copy-done.1, bf16[2560,128]{1,0:T(8,128)(2,1)} %copy-done.2), custom_call_target="tpu_custom_call" | custom-call | tf_op jit(solution)/shard_map/right/pallas_call | solution.py:128
  91.1 0.7 broadcast_in_dim.48
  91.8 12.8 %all_to_all.33 = f32[12,4,512]{2,1,0:T(4,128)S(1)} all-to-all(f32[12,4,512]{2,1,0:T(4,128)S(1)} %broadcast_in_dim.48), channel_id=1, replica_groups=mesh['rep_0'=12,'rep_1'=8,'rep_2'=2,'fsdp'=4] {'rep_0'}, dimensions={0} | all-to-all | bytes 196608 | tf_op jit(solution)/shard_map/all_to_all | solution.py:19
  104.7 14.2 %all_to_all.34.refs_0_ = f32[16,4,512]{2,1,0:T(4,128)} all-to-all(f32[16,4,512]{2,1,0:T(4,128)S(1)} %broadcast_in_dim.49), channel_id=1, replica_groups=mesh['rep_0'=12,'rep_1'=8,'rep_2'=2,'fsdp'=4] {'rep_1','rep_2'}, dimensions={0} | all-to-all | bytes 262144 | tf_op jit(solution)/shard_map/all_to_all | solution.py:19
  118.9 5.4 %last.1 = (bf16[2048,512]{1,0:T(8,128)(2,1)}, f32[4,512]{1,0:T(4,128)}) custom-call(f32[16,4,512]{2,1,0:T(4,128)} %all_to_all.34.refs_0_, f32[4,2048]{1,0:T(4,128)} %get-tuple-element.24.refs_1_, bf16[2560,128]{1,0:T(8,128)(2,1)} %get-tuple-element.15.refs_0_.refs_2_.refs_6_, bf16[2560,128]{1,0:T(8,128)(2,1)} %copy-done, bf16[2560,128]{1,0:T(8,128)(2,1)} %copy-done.1, ...), custom_call_target="tpu_custom_call" | custom-call | tf_op jit(solution)/shard_map/last/pallas_call | solution.py:170
  (5 shorter events, 0.1 us)
Async XLA Ops:
  1.9 9.6 %all-to-all-start = ((f32[4,4,512]{2,1,0:T(4,128)}), f32[4,4,512]{2,1,0:T(4,128)S(1)}, u32[]{:S(2)}, u32[]{:S(2)}) async-start(f32[4,4,512]{2,1,0:T(4,128)} %broadcast_in_dim.22), calls=%async_computation | async-start | bytes 65536 | tf_op jit(solution)/shard_map/all_to_all | solution.py:19
  11.5 30.6 %copy-start.4 = (bf16[2560,128]{1,0:T(8,128)(2,1)S(1)}, bf16[2560,128]{1,0:T(8,128)(2,1)}, u32[]{:S(2)}) copy-start(bf16[2560,128]{1,0:T(8,128)(2,1)} %get-tuple-element.21.refs_2_) | copy-start | bytes 1966084
  11.5 34.7 %copy-start.3 = (bf16[2560,128]{1,0:T(8,128)(2,1)S(1)}, bf16[2560,128]{1,0:T(8,128)(2,1)}, u32[]{:S(2)}) copy-start(bf16[2560,128]{1,0:T(8,128)(2,1)} %get-tuple-element.22.refs_3_) | copy-start | bytes 1966084
  11.5 0.6 copy-start.5
  39.9 45.0 %collective-permute-start = (bf16[2560,128]{1,0:T(8,128)(2,1)}, bf16[2560,128]{1,0:T(8,128)(2,1)S(1)}, u32[]{:S(2)}, u32[]{:S(2)}) collective-permute-start(bf16[2560,128]{1,0:T(8,128)(2,1)} %get-tuple-element.20.refs_1_), channel_id=1, source_target_pairs={{0,1},{1,2},{2,3},{3,0},{4,5},{5,6},{6,7},{7,4},{8,9},{9,10},{10,1... | collective-permute-start | bytes 1966088 | tf_op jit(solution)/shard_map/ppermute | solution.py:205
  42.1 42.7 %collective-permute-start.1 = (bf16[2560,128]{1,0:T(8,128)(2,1)S(1)}, bf16[2560,128]{1,0:T(8,128)(2,1)S(1)}, u32[]{:S(2)}, u32[]{:S(2)}) collective-permute-start(bf16[2560,128]{1,0:T(8,128)(2,1)S(1)} %copy-done.4), channel_id=1, source_target_pairs={{0,2},{1,3},{2,0},{3,1},{4,6},{5,7},{6,4},{7,5},{8,10},{9,11},{10,... | collective-permute-start | bytes 1966088 | tf_op jit(solution)/shard_map/ppermute | solution.py:205
  46.2 38.7 %collective-permute-start.2 = (bf16[2560,128]{1,0:T(8,128)(2,1)S(1)}, bf16[2560,128]{1,0:T(8,128)(2,1)S(1)}, u32[]{:S(2)}, u32[]{:S(2)}) collective-permute-start(bf16[2560,128]{1,0:T(8,128)(2,1)S(1)} %copy-done.3), channel_id=1, source_target_pairs={{0,3},{1,0},{2,1},{3,2},{4,7},{5,4},{6,5},{7,6},{8,11},{9,8},{10,9... | collective-permute-start | bytes 1966088 | tf_op jit(solution)/shard_map/ppermute | solution.py:205
  84.8 0.8 copy-start
  84.9 1.1 copy-start.1
  86.0 0.8 copy-start.2

commit v2 on v1

v2 whole, which is shorter than its diff:
```python
import jax
import jax.numpy as jnp
from jax import lax
from jax.experimental import pallas as pl
from jax.experimental.pallas import tpu as pltpu
from jax.sharding import Mesh
from jax.sharding import PartitionSpec as P

REP = ("rep_0", "rep_1", "rep_2")
REP_FSDP = ("rep_0", "rep_1", "rep_2", "fsdp")
VMEM = pl.BlockSpec(memory_space=pltpu.VMEM)
NN = (((1,), (0,)), ((), ()))
NT = (((1,), (1,)), ((), ()))
TN = (((0,), (0,)), ((), ()))
F32 = jnp.float32
BF16 = jnp.bfloat16


def exchange(array, axis):
    return lax.all_to_all(array, axis, 0, 0, tiled=True)


def sent_to_all(array, axis):
    return exchange(jnp.broadcast_to(array[None], (lax.axis_size(axis), *array.shape)), axis)


def pieces(value):
    first = value.astype(BF16)
    rest = value - first.astype(F32)
    second = rest.astype(BF16)
    third = (rest - second.astype(F32)).astype(BF16)
    return first, second, third


def exact_dot(value, short, dims):
    rows = value.shape[0]
    stacked = jnp.concatenate([p.astype(F32) for p in pieces(value)], axis=0).astype(BF16)
    out = lax.dot_general(stacked, short, dims, preferred_element_type=F32)
    return out[:rows] + (out[rows : 2 * rows] + out[2 * rows :])


def in_vmem(shape, dtype=F32):
    return pltpu.VMEM(shape, dtype)


def held(*arrays):
    return [pltpu.with_memory_space_constraint(array, pltpu.VMEM) for array in arrays]


def repeat_kernel(value_ref, out_ref):
    for k in range(out_ref.shape[0]):
        out_ref[k] = value_ref[...]


def repeated(value, times):
    return pl.pallas_call(
        repeat_kernel,
        in_specs=[VMEM],
        out_specs=VMEM,
        out_shape=in_vmem((times, *value.shape)),
        name="repeat",
    )(value)


def pack_kernel(me_ref, act_ref, up_ref, *refs):
    chunk_refs, sems = refs[:-1], refs[-1]
    groups = len(chunk_refs)
    rows = act_ref.shape[1] // groups
    copies = []
    for k, chunk_ref in enumerate(chunk_refs):
        start = pl.multiple_of(lax.rem(me_ref[0] + k, groups) * rows, rows)
        pairs = (
            (act_ref.at[:, pl.ds(start, rows)], chunk_ref.at[:, :rows]),
            (up_ref, chunk_ref.at[:, rows:]),
        )
        for i, (source, target) in enumerate(pairs):
            copies.append(pltpu.make_async_copy(source, target, sems.at[2 * k + i]))
    for copy in copies:
        copy.start()
    for copy in copies:
        copy.wait()


def packed(me, activations, upstream, groups):
    tok, width = activations.shape
    chunk = in_vmem((tok, width // groups + upstream.shape[1]), BF16)
    return pl.pallas_call(
        pack_kernel,
        in_specs=[pl.BlockSpec(memory_space=pltpu.SMEM)] + [pl.BlockSpec(memory_space=pl.ANY)] * 2,
        out_specs=[VMEM] * groups,
        out_shape=[chunk] * groups,
        scratch_shapes=[pltpu.SemaphoreType.DMA((2 * groups,))],
        name="pack",
    )(me, activations, upstream)


def left_kernel(me_ref, q_ref, *refs):
    chunk_refs, out_ref = refs[:-1], refs[-1]
    blocks, groups, rank, size = out_ref.shape
    rows = blocks * size
    ups = chunk_refs[0][:, rows:]
    for k in range(groups):
        g = lax.rem(me_ref[0] + k, groups)
        weights = exact_dot(q_ref[g], ups, NT)
        left = exact_dot(weights, chunk_refs[k][:, :rows], NN)
        for b in range(blocks):
            out_ref[b, g] = left[:, b * size : (b + 1) * size]


def left_parts(me, q_all, chunks, blocks):
    groups, rank, cols = q_all.shape
    rows = chunks[0].shape[1] - cols
    return pl.pallas_call(
        left_kernel,
        in_specs=[pl.BlockSpec(memory_space=pltpu.SMEM)] + [VMEM] * (groups + 1),
        out_specs=VMEM,
        out_shape=in_vmem((blocks, groups, rank, rows // blocks)),
        name="left",
    )(me, *held(q_all, *chunks))


def right_kernel(p_ref, *refs):
    chunk_refs, basis_ref, out_ref = refs[:-2], refs[-2], refs[-1]
    blocks, groups, rank, size = p_ref.shape
    rows = blocks * size
    basis = []
    for i in range(rank):
        vec = p_ref[:, 0, i, :]
        for g in range(1, groups):
            vec = vec + p_ref[:, g, i, :]
        for prev in basis:
            vec = vec - jnp.sum(vec * prev, keepdims=True) * prev
        vec = vec / jnp.sqrt(jnp.sum(vec * vec, keepdims=True) + 1e-06)
        basis.append(vec)
        for b in range(blocks):
            basis_ref[i : i + 1, b * size : (b + 1) * size] = vec[b : b + 1]
    whole = basis_ref[...]
    total = jnp.zeros(out_ref.shape[1:], F32)
    for chunk_ref in chunk_refs:
        weights = exact_dot(whole, chunk_ref[:, :rows], NT)
        total = total + exact_dot(weights, chunk_ref[:, rows:], NN)
    for k in range(out_ref.shape[0]):
        out_ref[k] = total


def basis_and_right(p_parts, chunks, copies):
    blocks, groups, rank, size = p_parts.shape
    rows = blocks * size
    return pl.pallas_call(
        right_kernel,
        in_specs=[VMEM] * (1 + groups),
        out_specs=[VMEM] * 2,
        out_shape=[
            in_vmem((rank, rows)),
            in_vmem((copies, rank, chunks[0].shape[1] - rows)),
        ],
        name="right",
    )(*held(p_parts, *chunks))


def error_and_factor(parts, basis, chunks, replicas):
    groups = len(chunks)
    rank, rows = basis.shape
    cols = chunks[0].shape[1] - rows
    steps = 4
    step_rows = rows // steps
    scale = 1.0 / replicas

    def kernel(parts_ref, basis_ref, *refs):
        chunk_refs = refs[:groups]
        error_ref, factor_ref, held_ref, sems = refs[groups:]
        factor = parts_ref[0]
        for part in range(1, parts_ref.shape[0]):
            factor = factor + parts_ref[part]
        factor_ref[...] = factor
        q0, q1, q2 = (p.astype(F32) for p in pieces(factor * scale))
        rights = jnp.concatenate([q0, q1, q0, q2, q1, q0], axis=0).astype(BF16)
        ups = jnp.concatenate([ref[:, rows:] for ref in chunk_refs], axis=0)
        copies = []
        for step in range(steps):
            span = slice(step * step_rows, (step + 1) * step_rows)
            acts = jnp.concatenate([ref[:, span] for ref in chunk_refs], axis=0)
            grad = lax.dot_general(acts, ups, TN, preferred_element_type=F32)
            b0, b1, b2 = (p.astype(F32) for p in pieces(basis_ref[:, span]))
            lefts = jnp.concatenate([b0, b0, b1, b0, b1, b2], axis=0).astype(BF16)
            approx = lax.dot_general(lefts, rights, TN, preferred_element_type=F32)
            held_ref[span] = (grad - approx).astype(BF16)
            copy = pltpu.make_async_copy(held_ref.at[span], error_ref.at[span], sems.at[step])
            copy.start()
            copies.append(copy)
        for copy in copies:
            copy.wait()

    return pl.pallas_call(
        kernel,
        in_specs=[VMEM] * (2 + groups),
        out_specs=[pl.BlockSpec(memory_space=pl.ANY), VMEM],
        out_shape=[
            jax.ShapeDtypeStruct((rows, cols), BF16),
            jax.ShapeDtypeStruct((rank, cols), F32),
        ],
        scratch_shapes=[
            pltpu.VMEM((rows, cols), BF16),
            pltpu.SemaphoreType.DMA((steps,)),
        ],
        name="last",
    )(*held(parts, basis, *chunks))


def on_device(activations, upstream, q_start):
    groups = lax.axis_size("fsdp")
    replicas = lax.axis_size(REP)
    planes = lax.axis_size("rep_0")
    pairs = ("rep_1", "rep_2")
    blocks = lax.axis_size(pairs)
    me = lax.axis_index("fsdp")[None]
    q_all = exchange(repeated(q_start[0], groups), "fsdp")
    chunks = packed(me, activations, upstream, groups)
    received = [chunks[0]] + [
        lax.ppermute(chunks[k], "fsdp", [(i, (i + k) % groups) for i in range(groups)])
        for k in range(1, groups)
    ]
    parts = exchange(left_parts(me, q_all, chunks, blocks), pairs)
    parts = sent_to_all(jnp.sum(parts, axis=0), "rep_0")
    parts = jnp.sum(parts, axis=0)
    parts = jnp.broadcast_to(parts[None], (blocks, *parts.shape))
    parts = exchange(parts.reshape(blocks * groups, *parts.shape[2:]), ("rep_1", "rep_2", "fsdp"))
    parts = parts.reshape(blocks, groups, *parts.shape[1:])
    p_basis, right = basis_and_right(parts, received, planes)
    right = jnp.sum(exchange(right, "rep_0"), axis=0)
    right_parts = sent_to_all(right, pairs)
    error_feedback, q_factor = error_and_factor(right_parts, p_basis, received, replicas)
    return (error_feedback[None], p_basis[None], q_factor[None])


def solution(mesh):
    split = Mesh(
        mesh.devices.reshape(12, 8, 2, mesh.shape["fsdp"]), ("rep_0", "rep_1", "rep_2", "fsdp")
    )
    return jax.shard_map(
        on_device,
        mesh=split,
        in_specs=(P(REP_FSDP, None), P(REP_FSDP, None), P("fsdp", None, None)),
        out_specs=(P(REP, "fsdp", None), P("fsdp", None, None), P("fsdp", None, None)),
        check_vma=False,
    )
```

time: 125 us -> 117 us (0.936)
  blocking collectives: 87.2 us -> 32.8 us
  starting transfers between devices: 13.8 us -> 45.7 us
  waiting for transfers between devices: 0.01 us -> 20.7 us
  Pallas kernels: 17.9 us -> 13.2 us
    all_to_all x5 -> x2, blocking collectives: 87.2 us -> 32.8 us  [exchange(): return lax.all_to_all(array, axis, 0, 0, tiled=True)]
    all_to_all x1 -> x4, starting transfers between devices: 4.83 us -> 37.1 us  [exchange(): return lax.all_to_all(array, axis, 0, 0, tiled=True)]
    all_to_all x1 -> x4, waiting for transfers between devices: 0.01 us -> 20.7 us  [exchange(): return lax.all_to_all(array, axis, 0, 0, tiled=True)]
    pallas_call x3 -> x4, Pallas kernels: 14.4 us -> 10.2 us  [the longest x1 3.26 us: error_and_factor(): pl.pallas_call(kernel, in_specs=[VMEM] * (2 + groups), out_specs=[pl.Bloc...]
    broadcast_in_dim x5 -> x2, local copies, waits for them, and re-layouts: 2.06 us -> 0.69 us  [sent_to_all(): jnp.broadcast_to(array[None], (lax.axis_size(axis), *array.shape))]
    unnamed x12 -> x5, local copies, waits for them, and re-layouts: 2.53 us -> 2.17 us
  transfers between devices with their start and end apart: 4 -> 7, of which waited for: 0 -> 4; matrix products, arithmetic and copies ran while one was open for 0% -> 1% of each run, Pallas kernels for 4% -> 2%
where the time goes in v2:
time: 117 us
  starting transfers between devices  45.7 us (39%)
  blocking collectives  32.8 us (28%)
  waiting for transfers between devices  20.7 us (18%)
  Pallas kernels  13.2 us (11%)
  local copies, waits for them, and re-layouts  3.53 us (3%)
    all_to_all x4, starting transfers between devices, exchange(): return lax.all_to_all(array, axis, 0, 0, tiled=True)  37.1 us
    all_to_all x2, blocking collectives, exchange(): return lax.all_to_all(array, axis, 0, 0, tiled=True)  32.8 us
    all_to_all x4, waiting for transfers between devices, exchange(): return lax.all_to_all(array, axis, 0, 0, tiled=True)  20.7 us
    ppermute x3, starting transfers between devices, on_device(): lax.ppermute(chunks[k], 'fsdp', [(i, (i + k) % groups) for i in range(gro...  8.59 us
    pallas_call x1, Pallas kernels, error_and_factor(): pl.pallas_call(kernel, in_specs=[VMEM] * (2 + groups), out_specs=[pl.Bloc...  3.26 us
    pallas_call x1, Pallas kernels, left_parts(): pl.pallas_call(left_kernel, in_specs=[pl.BlockSpec(memory_space=pltpu.SME...  2.97 us
    pallas_call x1, Pallas kernels, basis_and_right(): pl.pallas_call(right_kernel, in_specs=[VMEM] * (1 + groups), out_specs=[V...  2.83 us
    pallas_call x1, Pallas kernels, packed(): pl.pallas_call(pack_kernel, in_specs=[pl.BlockSpec(memory_space=pltpu.SME...  2.78 us
  transfers between devices with their start and end apart: 7, of which 4 were waited for; matrix products, arithmetic and copies ran while one was open for 1% of the time, Pallas kernels for 2%

profile of v2, /device:TPU:1, one launch (start us, length us, event | category | flops | bytes accessed | tf_op | source)
XLA Modules:
  0.0 116.6 jit_solution(8976099148507705258)
XLA Ops:
  0.6 1.3 %repeat.1 = f32[4,4,512]{2,1,0:T(4,128)} custom-call(f32[4,512]{1,0:T(4,128)} %bitcast.9), custom_call_target="tpu_custom_call" | custom-call | tf_op jit(solution)/shard_map/repeat/pallas_call | solution.py:56
  1.9 4.8 %all-to-all-start = ((f32[4,4,512]{2,1,0:T(4,128)}), f32[4,4,512]{2,1,0:T(4,128)S(1)}, u32[]{:S(2)}, u32[]{:S(2)}) async-start(f32[4,4,512]{2,1,0:T(4,128)} %repeat.1), calls=%async_computation | async-start | bytes 65536 | tf_op jit(solution)/shard_map/all_to_all | solution.py:20
  6.8 2.8 %pack.1 = (bf16[128,2560]{1,0:T(8,128)(2,1)S(1)}, bf16[128,2560]{1,0:T(8,128)(2,1)}, bf16[128,2560]{1,0:T(8,128)(2,1)}, bf16[128,2560]{1,0:T(8,128)(2,1)S(1)}) custom-call(s32[1]{0:T(128)} %bitcast.me_ref, bf16[128,8192]{1,0:T(8,128)(2,1)} %act_ref.1, bf16[128,512]{1,0:T(8,128)(2,1)} %up_ref.1), custom_call_target="tpu_custom_call" | custom-call | tf_op jit(solution)/shard_map/pack/pallas_call | solution.py:87
  9.6 1.5 %all-to-all-done.q_ref = f32[4,4,512]{2,1,0:T(4,128)S(1)} async-done(((f32[4,4,512]{2,1,0:T(4,128)}), f32[4,4,512]{2,1,0:T(4,128)S(1)}, u32[]{:S(2)}, u32[]{:S(2)}) %all-to-all-start) | async-done | bytes 32800 | tf_op jit(solution)/shard_map/all_to_all | solution.py:20
  11.1 3.0 %left.1 = f32[16,4,4,128]{3,2,1,0:T(4,128)} custom-call(s32[1]{0:T(128)} %bitcast.me_ref, f32[4,4,512]{2,1,0:T(4,128)S(1)} %all-to-all-done.q_ref, bf16[128,2560]{1,0:T(8,128)(2,1)S(1)} %get-tuple-element.11.refs_0_, bf16[128,2560]{1,0:T(8,128)(2,1)} %get-tuple-element.12.refs_1_, bf16[128,2560]{1,0:T(8,128)(2,1)} %get-tuple-element.13.refs_2_, ...), custom_call_target="tpu_custom_call" | custom-call | tf_op jit(solution)/shard_map/left/pallas_call | solution.py:113
  14.0 13.3 %all-to-all-start.1 = ((f32[16,4,4,128]{3,2,1,0:T(4,128)}), f32[16,4,4,128]{3,2,1,0:T(4,128)S(1)}, u32[]{:S(2)}, u32[]{:S(2)}) async-start(f32[16,4,4,128]{3,2,1,0:T(4,128)} %left.1), calls=%async_computation.1 | async-start | bytes 262144 | tf_op jit(solution)/shard_map/all_to_all | solution.py:20
  27.4 2.2 %collective-permute-start = (bf16[128,2560]{1,0:T(8,128)(2,1)}, bf16[128,2560]{1,0:T(8,128)(2,1)S(1)}, u32[]{:S(2)}, u32[]{:S(2)}) collective-permute-start(bf16[128,2560]{1,0:T(8,128)(2,1)} %get-tuple-element.12.refs_1_), channel_id=1, source_target_pairs={{0,1},{1,2},{2,3},{3,0},{4,5},{5,6},{6,7},{7,4},{8,9},{9,10},{10,1... | collective-permute-start | bytes 1966088 | tf_op jit(solution)/shard_map/ppermute | solution.py:220
  29.6 3.7 %collective-permute-start.1 = (bf16[128,2560]{1,0:T(8,128)(2,1)}, bf16[128,2560]{1,0:T(8,128)(2,1)S(1)}, u32[]{:S(2)}, u32[]{:S(2)}) collective-permute-start(bf16[128,2560]{1,0:T(8,128)(2,1)} %get-tuple-element.13.refs_2_), channel_id=1, source_target_pairs={{0,2},{1,3},{2,0},{3,1},{4,6},{5,7},{6,4},{7,5},{8,10},{9,11},{10,... | collective-permute-start | bytes 1966088 | tf_op jit(solution)/shard_map/ppermute | solution.py:220
  33.3 2.7 %collective-permute-start.2 = (bf16[128,2560]{1,0:T(8,128)(2,1)S(1)}, bf16[128,2560]{1,0:T(8,128)(2,1)S(1)}, u32[]{:S(2)}, u32[]{:S(2)}) collective-permute-start(bf16[128,2560]{1,0:T(8,128)(2,1)S(1)} %get-tuple-element.14.refs_3_), channel_id=1, source_target_pairs={{0,3},{1,0},{2,1},{3,2},{4,7},{5,4},{6,5},{7,6},{8,11},{9,8},{10,9... | collective-permute-start | bytes 1966088 | tf_op jit(solution)/shard_map/ppermute | solution.py:220
  36.0 0.6 all-to-all-done.1
  36.6 20.3 %all_to_all.30 = f32[12,4,4,128]{3,2,1,0:T(4,128)S(1)} all-to-all(f32[12,4,4,128]{3,2,1,0:T(4,128)S(1)} %broadcast_in_dim.15), channel_id=1, replica_groups=mesh['rep_0'=12,'rep_1'=8,'rep_2'=2,'fsdp'=4] {'rep_0'}, dimensions={0} | all-to-all | bytes 196608 | tf_op jit(solution)/shard_map/all_to_all | solution.py:20
  57.0 0.7 broadcast_in_dim.32
  57.6 12.1 %all-to-all-start.3 = ((f32[64,4,128]{2,1,0:T(4,128)}), f32[64,4,128]{2,1,0:T(4,128)S(1)}, u32[]{:S(2)}, u32[]{:S(2)}) async-start(f32[64,4,128]{2,1,0:T(4,128)} %bitcast.2), calls=%async_computation.3 | async-start | bytes 262144 | tf_op jit(solution)/shard_map/all_to_all | solution.py:20
  69.7 0.0 collective-permute-done.refs_1_
  69.7 0.0 collective-permute-done.1.refs_2_
  69.8 0.0 collective-permute-done.2.refs_3_
  69.8 10.0 %all-to-all-done.3 = f32[64,4,128]{2,1,0:T(4,128)S(1)} async-done(((f32[64,4,128]{2,1,0:T(4,128)}), f32[64,4,128]{2,1,0:T(4,128)S(1)}, u32[]{:S(2)}, u32[]{:S(2)}) %all-to-all-start.3) | async-done | bytes 131104 | tf_op jit(solution)/shard_map/all_to_all | solution.py:20
  79.8 0.0 copy-start
  79.8 0.7 copy-done
  80.4 0.0 copy-start.1
  80.4 0.9 copy-done.1
  81.3 2.8 %right.1 = (f32[4,2048]{1,0:T(4,128)S(1)}, f32[12,4,512]{2,1,0:T(4,128)S(1)}) custom-call(f32[16,4,4,128]{3,2,1,0:T(4,128)S(1)} %bitcast.8, bf16[128,2560]{1,0:T(8,128)(2,1)S(1)} %get-tuple-element.11.refs_0_, bf16[128,2560]{1,0:T(8,128)(2,1)S(1)} %collective-permute-done.refs_1_, bf16[128,2560]{1,0:T(8,128)(2,1)S(1)} %collective-permute-done.1.refs_2_, ...), custom_call_target="tpu_custom_call" | custom-call | tf_op jit(solution)/shard_map/right/pallas_call | solution.py:149
  84.2 12.5 %all_to_all.31 = f32[12,4,512]{2,1,0:T(4,128)S(1)} all-to-all(f32[12,4,512]{2,1,0:T(4,128)S(1)} %get-tuple-element.15), channel_id=1, replica_groups=mesh['rep_0'=12,'rep_1'=8,'rep_2'=2,'fsdp'=4] {'rep_0'}, dimensions={0} | all-to-all | bytes 196608 | tf_op jit(solution)/shard_map/all_to_all | solution.py:20
  96.7 0.7 broadcast_in_dim.33
  97.3 6.8 %all-to-all-start.5 = ((f32[16,4,512]{2,1,0:T(4,128)}), f32[16,4,512]{2,1,0:T(4,128)S(1)}, u32[]{:S(2)}, u32[]{:S(2)}) async-start(f32[16,4,512]{2,1,0:T(4,128)} %broadcast_in_dim.33), calls=%async_computation.5 | async-start | bytes 262144 | tf_op jit(solution)/shard_map/all_to_all | solution.py:20
  104.2 0.6 copy.6
  104.8 8.6 %all-to-all-done.5.parts_ref = f32[16,4,512]{2,1,0:T(4,128)S(1)} async-done(((f32[16,4,512]{2,1,0:T(4,128)}), f32[16,4,512]{2,1,0:T(4,128)S(1)}, u32[]{:S(2)}, u32[]{:S(2)}) %all-to-all-start.5) | async-done | bytes 131104 | tf_op jit(solution)/shard_map/all_to_all | solution.py:20
  113.3 3.3 %last.1 = (bf16[2048,512]{1,0:T(8,128)(2,1)}, f32[4,512]{1,0:T(4,128)}) custom-call(f32[16,4,512]{2,1,0:T(4,128)S(1)} %all-to-all-done.5.parts_ref, f32[4,2048]{1,0:T(4,128)S(1)} %get-tuple-element.16.basis_ref, bf16[128,2560]{1,0:T(8,128)(2,1)S(1)} %get-tuple-element.11.refs_0_, bf16[128,2560]{1,0:T(8,128)(2,1)S(1)} %collective-permute-done.refs_1_, ...), custom_call_target="tpu_custom_call" | custom-call | tf_op jit(solution)/shard_map/last/pallas_call | solution.py:194
  (4 shorter events, 0.1 us)
Async XLA Ops:
  1.9 9.1 %all-to-all-start = ((f32[4,4,512]{2,1,0:T(4,128)}), f32[4,4,512]{2,1,0:T(4,128)S(1)}, u32[]{:S(2)}, u32[]{:S(2)}) async-start(f32[4,4,512]{2,1,0:T(4,128)} %repeat.1), calls=%async_computation | async-start | bytes 65536 | tf_op jit(solution)/shard_map/all_to_all | solution.py:20
  14.0 22.5 %all-to-all-start.1 = ((f32[16,4,4,128]{3,2,1,0:T(4,128)}), f32[16,4,4,128]{3,2,1,0:T(4,128)S(1)}, u32[]{:S(2)}, u32[]{:S(2)}) async-start(f32[16,4,4,128]{3,2,1,0:T(4,128)} %left.1), calls=%async_computation.1 | async-start | bytes 262144 | tf_op jit(solution)/shard_map/all_to_all | solution.py:20
  27.4 42.4 %collective-permute-start = (bf16[128,2560]{1,0:T(8,128)(2,1)}, bf16[128,2560]{1,0:T(8,128)(2,1)S(1)}, u32[]{:S(2)}, u32[]{:S(2)}) collective-permute-start(bf16[128,2560]{1,0:T(8,128)(2,1)} %get-tuple-element.12.refs_1_), channel_id=1, source_target_pairs={{0,1},{1,2},{2,3},{3,0},{4,5},{5,6},{6,7},{7,4},{8,9},{9,10},{10,1... | collective-permute-start | bytes 1966088 | tf_op jit(solution)/shard_map/ppermute | solution.py:220
  29.6 40.2 %collective-permute-start.1 = (bf16[128,2560]{1,0:T(8,128)(2,1)}, bf16[128,2560]{1,0:T(8,128)(2,1)S(1)}, u32[]{:S(2)}, u32[]{:S(2)}) collective-permute-start(bf16[128,2560]{1,0:T(8,128)(2,1)} %get-tuple-element.13.refs_2_), channel_id=1, source_target_pairs={{0,2},{1,3},{2,0},{3,1},{4,6},{5,7},{6,4},{7,5},{8,10},{9,11},{10,... | collective-permute-start | bytes 1966088 | tf_op jit(solution)/shard_map/ppermute | solution.py:220
  33.3 36.5 %collective-permute-start.2 = (bf16[128,2560]{1,0:T(8,128)(2,1)S(1)}, bf16[128,2560]{1,0:T(8,128)(2,1)S(1)}, u32[]{:S(2)}, u32[]{:S(2)}) collective-permute-start(bf16[128,2560]{1,0:T(8,128)(2,1)S(1)} %get-tuple-element.14.refs_3_), channel_id=1, source_target_pairs={{0,3},{1,0},{2,1},{3,2},{4,7},{5,4},{6,5},{7,6},{8,11},{9,8},{10,9... | collective-permute-start | bytes 1966088 | tf_op jit(solution)/shard_map/ppermute | solution.py:220
  57.6 22.1 %all-to-all-start.3 = ((f32[64,4,128]{2,1,0:T(4,128)}), f32[64,4,128]{2,1,0:T(4,128)S(1)}, u32[]{:S(2)}, u32[]{:S(2)}) async-start(f32[64,4,128]{2,1,0:T(4,128)} %bitcast.2), calls=%async_computation.3 | async-start | bytes 262144 | tf_op jit(solution)/shard_map/all_to_all | solution.py:20
  79.8 0.7 copy-start
  80.4 0.9 copy-start.1
  97.3 16.0 %all-to-all-start.5 = ((f32[16,4,512]{2,1,0:T(4,128)}), f32[16,4,512]{2,1,0:T(4,128)S(1)}, u32[]{:S(2)}, u32[]{:S(2)}) async-start(f32[16,4,512]{2,1,0:T(4,128)} %broadcast_in_dim.33), calls=%async_computation.5 | async-start | bytes 262144 | tf_op jit(solution)/shard_map/all_to_all | solution.py:20
